TPU v7x, 32 devices: a whole 2x2x4 slice. The times are simulated.
32 devices in a mesh: grp: 2 (over x), req: 16 (over z, y, core).
Axes of the slice: x: 2, y: 2, z: 4, core: 2. Of those that a mesh axis runs over, the one named last changes fastest.
Arguments:
- moe_input: bfloat16 [512, 2048], P(('grp', 'req')), parts along dimension 0, may hold values from -6 to 6
- norm_gain: bfloat16 [2048], replicated, may hold values from 0.25 to 1.75
- route_ids: int32 [512, 8], P(('grp', 'req')), parts along dimension 0, may hold values from 0 to 15, all different within a row; in each aligned block of 16 rows (0 to 15, 16 to 31, ...) at most 16 rows name the same one
- route_gates: bfloat16 [512, 8], P(('grp', 'req')), parts along dimension 0, may hold values from 0.049804688 to 0.5
- expert_gate: bfloat16 [16, 2048, 768], P('req'), may hold values from -0.125 to 0.125
- expert_up: bfloat16 [16, 2048, 768], P('req'), may hold values from -0.125 to 0.125
- expert_down: bfloat16 [16, 768, 2048], P('req'), may hold values from -0.21875 to 0.21875
- queries: bfloat16 [128, 4096], P(('grp', 'req')), parts along dimension 0, may hold values from -4.5 to 4.5
- keys_cache: bfloat16 [128, 4, 384, 128], P(('grp', 'req')), parts along dimension 0, may hold values from -4.5 to 4.5
- values_cache: bfloat16 [128, 4, 384, 128], P(('grp', 'req')), parts along dimension 0, may hold values from -4.5 to 4.5
- new_keys: bfloat16 [128, 512], P(('grp', 'req')), parts along dimension 0, may hold values from -4.5 to 4.5
- new_values: bfloat16 [128, 512], P(('grp', 'req')), parts along dimension 0, may hold values from -4.5 to 4.5
- cache_lengths: int32 [128], P(('grp', 'req')), parts along dimension 0, may hold values from 1 to 384
Outputs:
- moe_out: bfloat16 [512, 2048], P(('grp', 'req')), parts along dimension 0
- attention_out: bfloat16 [128, 4096], P(('grp', 'req')), parts along dimension 0
There are 2 independent parts, one for each index of `grp`. A program takes and returns all parts, laid end to end along the dimension named above; an argument that names none is the same for every part. Nothing has to cross between parts.
Inputs may be any that keep to these rules, and one draw needn't show every extreme that they name: `route_ids`: each row names 8 different experts; in each aligned block of 16 rows (the rows of one device) no expert is named by more than 16 rows, a bound that some block reaches.
All inputs are finite; a program needn't handle non-finite values.
Results may differ from a plain program's by a relative error of at most 0.0065.
Values may be sent and summed in bfloat16 or wider, within the bound.
No kernel may reach another device: no remote copies, remote signals or barrier semaphores. Data moves between devices by JAX's collectives and lax.ppermute only.
A program may use at most 64 MiB of HBM per device.

v0:
```python
import jax
import jax.numpy as jnp
from jax import lax
from jax.sharding import PartitionSpec as P

EPS = 1e-06


def slot_table(route_ids, experts, capacity):
    onehot = (route_ids[:, :, None] == jnp.arange(experts, dtype=jnp.int32)[None, None, :]).astype(
        jnp.float32
    )
    present = jnp.sum(onehot, axis=1)
    earlier = jnp.cumsum(present, axis=0) - present
    levels = jnp.arange(capacity, dtype=jnp.float32)
    placed = present[:, :, None] * (earlier[:, :, None] == levels[None, None, :]).astype(
        jnp.float32
    )
    return (onehot, placed)


def expert_apply(received, w_gate, w_up, w_down):
    gate_part = jnp.einsum("nesd,edf->nesf", received, w_gate, preferred_element_type=jnp.float32)
    up_part = jnp.einsum("nesd,edf->nesf", received, w_up, preferred_element_type=jnp.float32)
    active = (jax.nn.silu(gate_part) * up_part).astype(jnp.bfloat16)
    return jnp.einsum("nesf,efd->nesd", active, w_down, preferred_element_type=jnp.float32).astype(
        jnp.bfloat16
    )


def attend(queries, keys_cache, values_cache, new_keys, new_values, cache_lengths):
    batch_rows = queries.shape[0]
    kv_heads = keys_cache.shape[1]
    cache_span = keys_cache.shape[2]
    head_size = keys_cache.shape[3]
    group_heads = queries.shape[1] // (kv_heads * head_size)
    score_scale = head_size ** (-0.5)
    grouped = queries.reshape(batch_rows, kv_heads, group_heads, head_size)
    scores = (
        jnp.einsum("bgqd,bgld->bgql", grouped, keys_cache, preferred_element_type=jnp.float32)
        * score_scale
    )
    own_score = (
        jnp.einsum(
            "bgqd,bgd->bgq",
            grouped,
            new_keys.reshape(batch_rows, kv_heads, head_size),
            preferred_element_type=jnp.float32,
        )
        * score_scale
    )
    live_mask = (jnp.arange(cache_span, dtype=jnp.int32)[None, :] < cache_lengths[:, None])[
        :, None, None, :
    ]
    highest = jnp.maximum(jnp.max(jnp.where(live_mask, scores, -jnp.inf), axis=-1), own_score)
    weights = jnp.where(live_mask, jnp.exp(scores - highest[..., None]), 0.0)
    own_weight = jnp.exp(own_score - highest)
    totals = jnp.sum(weights, axis=-1) + own_weight
    prob_low = (weights / totals[..., None]).astype(jnp.bfloat16)
    own_prob = (own_weight / totals).astype(jnp.bfloat16)
    mixed_out = jnp.einsum(
        "bgql,bgld->bgqd", prob_low, values_cache, preferred_element_type=jnp.float32
    )
    mixed_out = mixed_out + own_prob.astype(jnp.float32)[..., None] * new_values.reshape(
        batch_rows, kv_heads, 1, head_size
    ).astype(jnp.float32)
    return mixed_out.reshape(batch_rows, -1).astype(jnp.bfloat16)


def body(
    moe_input,
    norm_gain,
    route_ids,
    route_gates,
    expert_gate,
    expert_up,
    expert_down,
    queries,
    keys_cache,
    values_cache,
    new_keys,
    new_values,
    cache_lengths,
):
    row_count = moe_input.shape[0]
    model_width = moe_input.shape[1]
    local_experts = expert_gate.shape[0]
    devices = lax.axis_size("req")
    experts = devices * local_experts
    capacity = min(row_count, max(2, 16 * row_count // experts))
    hidden = moe_input.astype(jnp.float32)
    normed = (
        hidden
        * lax.rsqrt(jnp.mean(hidden * hidden, axis=-1, keepdims=True) + EPS)
        * norm_gain.astype(jnp.float32)
    ).astype(jnp.bfloat16)
    onehot, placed = slot_table(route_ids, experts, capacity)
    selector = placed.reshape(row_count, experts * capacity).astype(jnp.bfloat16)
    outgoing = jnp.einsum("rs,rd->sd", selector, normed, preferred_element_type=jnp.float32).astype(
        jnp.bfloat16
    )
    outgoing = outgoing.reshape(devices, local_experts, capacity, model_width)
    produced = expert_apply(
        lax.all_to_all(outgoing, "req", split_axis=0, concat_axis=0, tiled=True),
        expert_gate,
        expert_up,
        expert_down,
    )
    returned = lax.all_to_all(produced, "req", split_axis=0, concat_axis=0, tiled=True)
    weight = jnp.einsum("rke,rk->re", onehot, route_gates.astype(jnp.float32))
    combine = (
        (weight[:, :, None] * placed).reshape(row_count, experts * capacity).astype(jnp.bfloat16)
    )
    expert_sum = jnp.dot(
        combine,
        returned.reshape(experts * capacity, model_width),
        preferred_element_type=jnp.float32,
    )
    moe_out = (hidden + expert_sum).astype(jnp.bfloat16)
    attention_out = attend(queries, keys_cache, values_cache, new_keys, new_values, cache_lengths)
    return (moe_out, attention_out)


def solution(mesh):
    in_specs = (
        P(("grp", "req"), None),
        P(),
        P(("grp", "req"), None),
        P(("grp", "req"), None),
        P("req", None, None),
        P("req", None, None),
        P("req", None, None),
        P(("grp", "req"), None),
        P(("grp", "req"), None, None, None),
        P(("grp", "req"), None, None, None),
        P(("grp", "req"), None),
        P(("grp", "req"), None),
        P(("grp", "req")),
    )
    out_specs = (P(("grp", "req"), None), P(("grp", "req"), None))
    return jax.shard_map(body, mesh=mesh, in_specs=in_specs, out_specs=out_specs, check_vma=False)
```

profile of v0, /device:TPU:9, one launch (start us, length us, event | category | flops | bytes accessed | tf_op | source)
XLA Modules:
  0.0 79.6 jit_solution(15654762199548620591)
XLA Ops:
  0.6 0.0 copy-start
  0.6 0.0 copy-start.5
  0.7 0.9 %copy.19 = s32[16,8]{1,0:T(8,128)S(1)} copy(s32[16,8]{0,1:T(8,128)} %param.15) | data formatting | bytes 1024 | tf_op args[2]
  1.6 0.1 convert_reduce_fusion
  1.7 0.7 convert_element_type.81
  2.4 1.0 %fusion.38 = f32[16]{0:T(128)S(1)} fusion(bf16[16,2048]{1,0:T(8,128)(2,1)} %param.13), kind=kLoop, calls=%fused_computation.29 | loop fusion | flops 98288 | bytes 65600 | tf_op jit(solution)/shard_map/reduce_sum | solution.py:94
  3.4 0.1 mul.80
  3.5 0.1 mul.83
  3.6 0.1 eq.48
  3.7 0.1 eq.51
  3.8 0.1 eq.53
  3.9 2.4 %convolution_convert_fusion = bf16[256,2048]{1,0:T(8,128)(2,1)} fusion(bf16[16,2048]{1,0:T(8,128)(2,1)} %param.13, f32[2048]{0:T(1024)S(1)} %convert_element_type.81, f32[16]{0:T(128)S(1)} %add_rsqrt_fusion, bf16[16,256]{1,0:T(8,128)(2,1)S(1)} %mul.83, f32[16,256]{1,0:T(8,128)S(1)} %eq.51, f32[256]{0:T(256)S(1)} %eq.53), kind=kOutput, calls=%fused_computation.7 | convolution fusion | flops 17440768 | bytes 1147968 | tf_op jit(solution)/shard_map/rs,rd->sd/dot_general | solution.py:99
  6.3 6.6 %all-to-all-start = ((bf16[16,1,16,2048]{3,2,1,0:T(8,128)(2,1)}), bf16[16,1,16,2048]{3,2,1,0:T(8,128)(2,1)}, u32[]{:S(2)}, u32[]{:S(2)}) async-start(bf16[16,1,16,2048]{3,2,1,0:T(8,128)(2,1)} %bitcast.97), calls=%async_computation | async-start | bytes 2097152 | tf_op jit(solution)/shard_map/all_to_all | solution.py:104
  12.8 0.0 copy-done.5
  12.9 0.1 copy.22
  12.9 24.9 %all-to-all-done = bf16[16,1,16,2048]{3,2,1,0:T(8,128)(2,1)} async-done(((bf16[16,1,16,2048]{3,2,1,0:T(8,128)(2,1)}), bf16[16,1,16,2048]{3,2,1,0:T(8,128)(2,1)}, u32[]{:S(2)}, u32[]{:S(2)}) %all-to-all-start) | async-done | bytes 1048608 | tf_op jit(solution)/shard_map/all_to_all | solution.py:104
  37.9 4.1 %fusion.13 = f32[16,1,16,768]{3,2,0,1:T(8,128)} fusion(bf16[1,2048,768]{2,1,0:T(8,128)(2,1)} %param.17, bf16[16,1,16,2048]{3,2,1,0:T(8,128)(2,1)} %all-to-all-done), kind=kOutput, calls=%fused_computation.11 | convolution fusion | flops 805306368 | bytes 4980736 | tf_op jit(solution)/shard_map/nesd,edf->nesf/dot_general | solution.py:23
  42.0 0.0 copy-done
  42.0 0.0 copy-start.3
  42.0 0.0 copy-start.4
  42.0 0.0 copy-start.6
  42.0 0.0 copy-start.2
  42.0 5.6 %fusion.9 = bf16[16,1,16,2048]{3,2,1,0:T(8,128)(2,1)} fusion(bf16[1,768,2048]{2,1,0:T(8,128)(2,1)S(1)} %copy-done, bf16[1,2048,768]{2,1,0:T(8,128)(2,1)} %param.18, bf16[16,1,16,2048]{3,2,1,0:T(8,128)(2,1)} %all-to-all-done, f32[16,1,16,768]{3,2,0,1:T(8,128)} %fusion.13), kind=kOutput, calls=%fused_computation.8 | convolution fusion | flops 1612316672 | bytes 9175040 | tf_op jit(solution)/shard_map/nesf,efd->nesd/dot_general | solution.py:26
  47.6 0.0 copy-start.1
  47.6 4.9 %all-to-all-start.1 = ((bf16[16,1,16,2048]{3,2,1,0:T(8,128)(2,1)}), bf16[16,1,16,2048]{3,2,1,0:T(8,128)(2,1)}, u32[]{:S(2)}, u32[]{:S(2)}) async-start(bf16[16,1,16,2048]{3,2,1,0:T(8,128)(2,1)} %fusion.9), calls=%async_computation.1 | async-start | bytes 2097152 | tf_op jit(solution)/shard_map/all_to_all | solution.py:109
  52.5 0.2 fusion.48
  52.7 0.2 multiply_convert_fusion
  52.9 0.1 convert_element_type.79
  53.0 0.0 copy-done.3
  53.0 0.0 copy-done.4
  53.0 0.0 copy-done.6
  53.1 0.1 iota_compare_fusion.3
  53.1 0.0 copy-done.2
  53.1 0.1 fusion.49
  53.3 2.1 %select_reduce_fusion = (f32[4,4,8]{2,1,0:T(4,128)S(1)}, f32[4,4,8,384]{3,2,1,0:T(8,128)S(1)}) fusion(pred[4,384]{1,0:T(4,128)(4,1)S(1)} %iota_compare_fusion.3, bf16[4,4,384,128]{3,2,1,0:T(8,128)(2,1)} %param.21, bf16[1,4,32,128]{3,1,2,0:T(4,128)(2,1)S(1)} %bitcast.102), kind=kOutput, calls=%fused_computation.25 | convolution fusion | flops 12730240 | bytes 1804288 | tf_op jit(solution)/shard_map/bgqd,bgld->bgql/dot_general | solution.py:40
  55.4 0.2 fusion.37
  55.7 1.8 %fusion.29 = bf16[1,4,32,128]{3,2,1,0:T(8,128)(2,1)S(1)} fusion(bf16[4,4,384,128]{3,2,1,0:T(8,128)(2,1)} %param.22, f32[4,4,8,384]{3,2,1,0:T(8,128)S(1)} %get-tuple-element.5, f32[4,4,8]{2,1,0:T(4,128)S(1)} %get-tuple-element.3, f32[4,4,8]{2,1,0:T(4,128)S(1)} %multiply_maximum_fusion, pred[4,384]{1,0:T(4,128)(4,1)S(1)} %iota_compare_fusion.3, ...), kind=kOutput, calls=%fused_computation.19 | convolution fusion | flops 12828672 | bytes 1813504 | tf_op jit(solution)/shard_map/bgql,bgld->bgqd/dot_general | solution.py:61
  57.5 0.7 copy.39
  58.1 19.4 %all-to-all-done.1 = bf16[16,1,16,2048]{3,2,1,0:T(8,128)(2,1)} async-done(((bf16[16,1,16,2048]{3,2,1,0:T(8,128)(2,1)}), bf16[16,1,16,2048]{3,2,1,0:T(8,128)(2,1)}, u32[]{:S(2)}, u32[]{:S(2)}) %all-to-all-start.1) | async-done | bytes 1048608 | tf_op jit(solution)/shard_map/all_to_all | solution.py:109
  77.5 0.0 copy-done.1
  77.5 2.1 %fusion.12 = bf16[16,2048]{1,0:T(8,128)(2,1)} fusion(bf16[16,256]{1,0:T(8,128)(2,1)S(1)} %convert_element_type.79, bf16[256,2048]{1,0:T(8,128)(2,1)} %bitcast.25, bf16[16,2048]{1,0:T(8,128)(2,1)S(1)} %copy-done.1), kind=kOutput, calls=%fused_computation.10 | convolution fusion | flops 16875520 | bytes 1187840 | tf_op jit(solution)/shard_map/dot_general | solution.py:114
  (8 shorter events, 0.1 us)
Async XLA Ops:
  0.6 41.3 %copy-start = (bf16[1,768,2048]{2,1,0:T(8,128)(2,1)S(1)}, bf16[1,768,2048]{2,1,0:T(8,128)(2,1)}, u32[]{:S(2)}) copy-start(bf16[1,768,2048]{2,1,0:T(8,128)(2,1)} %param.19) | copy-start | bytes 9437188
  0.6 12.2 %copy-start.5 = (bf16[16,8]{0,1:T(8,128)(2,1)S(1)}, bf16[16,8]{0,1:T(8,128)(2,1)}, u32[]{:S(2)}) copy-start(bf16[16,8]{0,1:T(8,128)(2,1)} %param.16) | copy-start | bytes 772
  6.3 31.6 %all-to-all-start = ((bf16[16,1,16,2048]{3,2,1,0:T(8,128)(2,1)}), bf16[16,1,16,2048]{3,2,1,0:T(8,128)(2,1)}, u32[]{:S(2)}, u32[]{:S(2)}) async-start(bf16[16,1,16,2048]{3,2,1,0:T(8,128)(2,1)} %bitcast.97), calls=%async_computation | async-start | bytes 2097152 | tf_op jit(solution)/shard_map/all_to_all | solution.py:104
  42.0 11.0 %copy-start.3 = (bf16[4,512]{1,0:T(4,128)(2,1)S(1)}, bf16[4,512]{1,0:T(4,128)(2,1)}, u32[]{:S(2)}) copy-start(bf16[4,512]{1,0:T(4,128)(2,1)} %param.23) | copy-start | bytes 12292
  42.0 11.0 %copy-start.4 = (bf16[4,512]{1,0:T(4,128)(2,1)S(1)}, bf16[4,512]{1,0:T(4,128)(2,1)}, u32[]{:S(2)}) copy-start(bf16[4,512]{1,0:T(4,128)(2,1)} %param.24) | copy-start | bytes 12292
  42.0 11.1 %copy-start.6 = (s32[4]{0:T(128)S(1)}, s32[4]{0:T(128)}, u32[]{:S(2)}) copy-start(s32[4]{0:T(128)} %param.25) | copy-start | bytes 52
  42.0 11.1 %copy-start.2 = (bf16[4,4096]{1,0:T(4,128)(2,1)S(1)}, bf16[4,4096]{1,0:T(4,128)(2,1)}, u32[]{:S(2)}) copy-start(bf16[4,4096]{1,0:T(4,128)(2,1)} %param.20) | copy-start | bytes 98308
  47.6 29.9 %copy-start.1 = (bf16[16,2048]{1,0:T(8,128)(2,1)S(1)}, bf16[16,2048]{1,0:T(8,128)(2,1)}, u32[]{:S(2)}) copy-start(bf16[16,2048]{1,0:T(8,128)(2,1)} %param.13) | copy-start | bytes 196612
  47.6 29.9 %all-to-all-start.1 = ((bf16[16,1,16,2048]{3,2,1,0:T(8,128)(2,1)}), bf16[16,1,16,2048]{3,2,1,0:T(8,128)(2,1)}, u32[]{:S(2)}, u32[]{:S(2)}) async-start(bf16[16,1,16,2048]{3,2,1,0:T(8,128)(2,1)} %fusion.9), calls=%async_computation.1 | async-start | bytes 2097152 | tf_op jit(solution)/shard_map/all_to_all | solution.py:109
where the time goes:
time: 80.1 us; the launch traced here: 79.6 us
  waiting for transfers between devices  44.3 us (55%)
  matrix products  18.5 us (23%)
  starting transfers between devices  11.5 us (14%)
  local copies, waits for them, and re-layouts  2.34 us (3%)
  other arithmetic  2.27 us (3%)
    all_to_all x1, waiting for transfers between devices, body(): lax.all_to_all(outgoing, 'req', split_axis=0, concat_axis=0, tiled=True)  24.9 us
    all_to_all x1, waiting for transfers between devices, body(): lax.all_to_all(produced, 'req', split_axis=0, concat_axis=0, tiled=True)  19.4 us
    all_to_all x1, starting transfers between devices, body(): lax.all_to_all(outgoing, 'req', split_axis=0, concat_axis=0, tiled=True)  6.58 us
    dot_general x1, matrix products, expert_apply(): jnp.einsum('nesf,efd->nesd', active, w_down, preferred_element_type=jnp.f...  5.59 us
    all_to_all x1, starting transfers between devices, body(): lax.all_to_all(produced, 'req', split_axis=0, concat_axis=0, tiled=True)  4.89 us
    dot_general x1, matrix products, expert_apply(): jnp.einsum('nesd,edf->nesf', received, w_gate, preferred_element_type=jnp...  4.1 us
    dot_general x1, matrix products, body(): jnp.einsum('rs,rd->sd', selector, normed, preferred_element_type=jnp.floa...  2.35 us
    dot_general x1, matrix products, attend(): jnp.einsum('bgqd,bgld->bgql', grouped, keys_cache, preferred_element_type...  2.15 us
  transfers between devices with their start and end apart: 2, of which 2 were waited for; matrix products, arithmetic and copies ran while one was open for 7% of the time, Pallas kernels for 0%

commit v1 on v0

--- a/solution.py
+++ b/solution.py
@@ -1,9 +1,130 @@
+import functools
 import jax
 import jax.numpy as jnp
 from jax import lax
+from jax.experimental import pallas as pl
+from jax.experimental.pallas import tpu as pltpu
 from jax.sharding import PartitionSpec as P
 
 EPS = 1e-06
+LANES = 128
+
+
+def pack_kernel(hidden_ref, gain_ref, ids_ref, gates_ref, packed_ref):
+    rows, width = hidden_ref.shape
+    lanes = packed_ref.shape[1] - width
+    hidden = hidden_ref[...].astype(jnp.float32)
+    scale = lax.rsqrt(jnp.mean(hidden * hidden, axis=-1, keepdims=True) + EPS)
+    packed_ref[:, :width] = (hidden * scale * gain_ref[...].astype(jnp.float32)).astype(jnp.bfloat16)
+    expert = lax.broadcasted_iota(jnp.int32, (lanes, rows), 0)
+    weight = jnp.zeros((lanes, rows), jnp.float32)
+    for k in range(ids_ref.shape[0]):
+        gate = gates_ref[k : k + 1, :].astype(jnp.float32)
+        weight = weight + jnp.where(ids_ref[k : k + 1, :] == expert, gate, 0.0)
+    row = lax.broadcasted_iota(jnp.int32, (rows, rows), 0)
+    column = lax.broadcasted_iota(jnp.int32, (rows, rows), 1)
+    packed_ref[:, width:] = lax.dot_general(
+        (row == column).astype(jnp.bfloat16),
+        weight.astype(jnp.bfloat16),
+        (((1,), (1,)), ((), ())),
+        preferred_element_type=jnp.float32,
+    ).astype(jnp.bfloat16)
+
+
+def pack(moe_input, norm_gain, route_ids, route_gates, experts):
+    rows, width = moe_input.shape
+    lanes = -(-experts // LANES) * LANES
+    return pl.pallas_call(
+        pack_kernel,
+        out_shape=jax.ShapeDtypeStruct((rows, width + lanes), jnp.bfloat16),
+        name="pack",
+        compiler_params=pltpu.CompilerParams(vmem_limit_bytes=2 << 20),
+        cost_estimate=pl.CostEstimate(flops=rows * width * 8, bytes_accessed=rows * width * 4, transcendentals=rows),
+    )(moe_input, norm_gain.reshape(1, width), route_ids.T, route_gates.T)
+
+
+def expert_kernel(first_ref, second_ref, gate_ref, up_ref, down_ref, kept_ref, sent_ref, total_ref):
+    step = pl.program_id(0)
+    width = gate_ref.shape[1]
+    half = first_ref.shape[0]
+    rows = jnp.concatenate([first_ref[:, :width], second_ref[:, :width]], axis=0)
+    gate_part = jnp.dot(rows, gate_ref[0], preferred_element_type=jnp.float32)
+    up_part = jnp.dot(rows, up_ref[0], preferred_element_type=jnp.float32)
+    active = (gate_part / (1.0 + jnp.exp(-gate_part)) * up_part).astype(jnp.bfloat16)
+    part = jnp.dot(active, down_ref[0], preferred_element_type=jnp.float32)
+
+    @pl.when(step == 0)
+    def _():
+        total_ref[...] = part
+
+    @pl.when(step > 0)
+    def _():
+        total_ref[...] += part
+
+    @pl.when(step == pl.num_programs(0) - 1)
+    def _():
+        expert = lax.axis_index("req")
+        for source, target, base in ((first_ref, kept_ref, 0), (second_ref, sent_ref, half)):
+            weights = source[:, width:].astype(jnp.float32)
+            mine = lax.broadcasted_iota(jnp.int32, weights.shape, 1) == expert
+            weight = jnp.sum(jnp.where(mine, weights, 0.0), axis=1, keepdims=True)
+            produced = total_ref[base : base + half, :].astype(jnp.bfloat16).astype(jnp.float32)
+            target[...] = (produced * weight).astype(target.dtype)
+
+
+def expert_section(first, second, w_gate, w_up, w_down):
+    half, packed = first.shape
+    _, width, hidden = w_gate.shape
+    tile = 256 if hidden % 256 == 0 else hidden
+    steps = hidden // tile
+    return pl.pallas_call(
+        expert_kernel,
+        grid=(steps,),
+        in_specs=[
+            pl.BlockSpec((half, packed), lambda j: (0, 0)),
+            pl.BlockSpec((half, packed), lambda j: (0, 0)),
+            pl.BlockSpec((1, width, tile), lambda j: (0, 0, j)),
+            pl.BlockSpec((1, width, tile), lambda j: (0, 0, j)),
+            pl.BlockSpec((1, tile, width), lambda j: (0, j, 0)),
+        ],
+        out_specs=[
+            pl.BlockSpec((half, width), lambda j: (0, 0)),
+            pl.BlockSpec((half, width), lambda j: (0, 0)),
+        ],
+        out_shape=[
+            jax.ShapeDtypeStruct((half, width), jnp.float32),
+            jax.ShapeDtypeStruct((half, width), jnp.bfloat16),
+        ],
+        scratch_shapes=[pltpu.VMEM((2 * half, width), jnp.float32)],
+        name="experts",
+        compiler_params=pltpu.CompilerParams(vmem_limit_bytes=32 << 20),
+        cost_estimate=pl.CostEstimate(
+            flops=12 * half * width * hidden,
+            bytes_accessed=6 * width * hidden + 8 * half * width,
+            transcendentals=2 * half * hidden,
+        ),
+    )(first, second, w_gate, w_up, w_down)
+
+
+def exchange(value, distance, devices):
+    return lax.ppermute(value, "req", [(i, i ^ distance) for i in range(devices)])
+
+
+def gathered_layer(packed, w_gate, w_up, w_down, hidden, devices):
+    rows, width = hidden.shape
+    far = range(4, devices, 4)
+    column = jnp.concatenate([packed] + [exchange(packed, k, devices) for k in far], axis=0)
+    plane = jnp.concatenate([column, exchange(column, 2, devices)], axis=0)
+    other = exchange(plane, 1, devices)
+    kept, sent = expert_section(plane, other, w_gate, w_up, w_down)
+    kept = kept + exchange(sent, 1, devices).astype(jnp.float32)
+    half = kept.shape[0] // 2
+    kept = kept[:half] + exchange(kept[half:].astype(jnp.bfloat16), 2, devices).astype(jnp.float32)
+    total = hidden.astype(jnp.float32) + kept[:rows]
+    for i, k in enumerate(far):
+        block = kept[(i + 1) * rows : (i + 2) * rows].astype(jnp.bfloat16)
+        total = total + exchange(block, k, devices).astype(jnp.float32)
+    return total.astype(jnp.bfloat16)
 
 
 def slot_table(route_ids, experts, capacity):
@@ -65,6 +186,46 @@
         batch_rows, kv_heads, 1, head_size
     ).astype(jnp.float32)
     return mixed_out.reshape(batch_rows, -1).astype(jnp.bfloat16)
+
+
+def slotted_layer(
+    moe_input, norm_gain, route_ids, route_gates, expert_gate, expert_up, expert_down, capacity
+):
+    row_count = moe_input.shape[0]
+    model_width = moe_input.shape[1]
+    local_experts = expert_gate.shape[0]
+    devices = lax.axis_size("req")
+    experts = devices * local_experts
+    hidden = moe_input.astype(jnp.float32)
+    normed = (
+        hidden
+        * lax.rsqrt(jnp.mean(hidden * hidden, axis=-1, keepdims=True) + EPS)
+        * norm_gain.astype(jnp.float32)
+    ).astype(jnp.bfloat16)
+    onehot, placed = slot_table(route_ids, experts, capacity)
+    selector = placed.reshape(row_count, experts * capacity).astype(jnp.bfloat16)
+    outgoing = jnp.einsum("rs,rd->sd", selector, normed, preferred_element_type=jnp.float32).astype(
+        jnp.bfloat16
+    )
+    outgoing = outgoing.reshape(devices, local_experts, capacity, model_width)
+    produced = expert_apply(
+        lax.all_to_all(outgoing, "req", split_axis=0, concat_axis=0, tiled=True),
+        expert_gate,
+        expert_up,
+        expert_down,
+    )
+    returned = lax.all_to_all(produced, "req", split_axis=0, concat_axis=0, tiled=True)
+    weight = jnp.einsum("rke,rk->re", onehot, route_gates.astype(jnp.float32))
+    combine = (
+        (weight[:, :, None] * placed).reshape(row_count, experts * capacity).astype(jnp.bfloat16)
+    )
+    expert_sum = jnp.dot(
+        combine,
+        returned.reshape(experts * capacity, model_width),
+        preferred_element_type=jnp.float32,
+    )
+    moe_out = (hidden + expert_sum).astype(jnp.bfloat16)
+    return moe_out
 
 
 def body(
@@ -88,35 +249,13 @@
     devices = lax.axis_size("req")
     experts = devices * local_experts
     capacity = min(row_count, max(2, 16 * row_count // experts))
-    hidden = moe_input.astype(jnp.float32)
-    normed = (
-        hidden
-        * lax.rsqrt(jnp.mean(hidden * hidden, axis=-1, keepdims=True) + EPS)
-        * norm_gain.astype(jnp.float32)
-    ).astype(jnp.bfloat16)
-    onehot, placed = slot_table(route_ids, experts, capacity)
-    selector = placed.reshape(row_count, experts * capacity).astype(jnp.bfloat16)
-    outgoing = jnp.einsum("rs,rd->sd", selector, normed, preferred_element_type=jnp.float32).astype(
-        jnp.bfloat16
-    )
-    outgoing = outgoing.reshape(devices, local_experts, capacity, model_width)
-    produced = expert_apply(
-        lax.all_to_all(outgoing, "req", split_axis=0, concat_axis=0, tiled=True),
-        expert_gate,
-        expert_up,
-        expert_down,
-    )
-    returned = lax.all_to_all(produced, "req", split_axis=0, concat_axis=0, tiled=True)
-    weight = jnp.einsum("rke,rk->re", onehot, route_gates.astype(jnp.float32))
-    combine = (
-        (weight[:, :, None] * placed).reshape(row_count, experts * capacity).astype(jnp.bfloat16)
-    )
-    expert_sum = jnp.dot(
-        combine,
-        returned.reshape(experts * capacity, model_width),
-        preferred_element_type=jnp.float32,
-    )
-    moe_out = (hidden + expert_sum).astype(jnp.bfloat16)
+    if local_experts == 1 and capacity == row_count and devices >= 8 and devices & (devices - 1) == 0:
+        packed = pack(moe_input, norm_gain, route_ids, route_gates, experts)
+        moe_out = gathered_layer(packed, expert_gate, expert_up, expert_down, moe_input, devices)
+    else:
+        moe_out = slotted_layer(
+            moe_input, norm_gain, route_ids, route_gates, expert_gate, expert_up, expert_down, capacity
+        )
     attention_out = attend(queries, keys_cache, values_cache, new_keys, new_values, cache_lengths)
     return (moe_out, attention_out)
 

time: 80.1 us -> 55.2 us (0.69)
  the two profiles are of different devices: /device:TPU:9 before, /device:TPU:0 now
where the time goes in v1:
time: 55.2 us; the launch traced here: 54.8 us
  waiting for transfers between devices  23.8 us (43%)
  starting transfers between devices  13.6 us (25%)
  local copies, waits for them, and re-layouts  9.52 us (17%)
  Pallas kernels  4.67 us (8%)
  matrix products  1.28 us (2%)
  other arithmetic  1.15 us (2%)
  between operations  0.78 us (1%)
    ppermute x10, waiting for transfers between devices, exchange(): lax.ppermute(value, 'req', [(i, i ^ distance) for i in range(devices)])  23.8 us
    ppermute x10, starting transfers between devices, exchange(): lax.ppermute(value, 'req', [(i, i ^ distance) for i in range(devices)])  13.6 us
    unnamed x31, local copies, waits for them, and re-layouts  8.61 us
    pallas_call x1, Pallas kernels, expert_section(): pl.pallas_call(expert_kernel, grid=(steps,), in_specs=[pl.BlockSpec((half...  4.49 us
  transfers between devices with their start and end apart: 10, of which 7 were waited for; matrix products, arithmetic and copies ran while one was open for 4% of the time, Pallas kernels for 0%

profile of v1, /device:TPU:0, one launch (start us, length us, event | category | flops | bytes accessed | tf_op | source)
XLA Modules:
  0.0 54.8 jit_solution(14310226283558699337)
XLA Ops:
  0.6 0.0 copy-start
  0.6 0.0 copy-start.9
  0.7 0.8 %reshape.45.gain_ref = bf16[1,2048]{1,0:T(2,128)(2,1)S(1)} reshape(bf16[2048]{0:T(1024)(128)(2,1)} %param.14) | data formatting | bytes 8192 | tf_op jit(solution)/shard_map/reshape | solution.py:43
  1.5 0.0 copy-start.4
  1.5 0.8 %copy-done.4 = bf16[16,2048]{1,0:T(8,128)(2,1)S(1)} copy-done((bf16[16,2048]{1,0:T(8,128)(2,1)S(1)}, bf16[16,2048]{1,0:T(8,128)(2,1)}, u32[]{:S(2)}) %copy-start.4) | copy-done | bytes 65560
  2.3 0.0 copy-start.6
  2.3 0.7 %copy-done.6 = s32[16,8]{0,1:T(8,128)S(1)} copy-done((s32[16,8]{0,1:T(8,128)S(1)}, s32[16,8]{0,1:T(8,128)}, u32[]{:S(2)}) %copy-start.6) | copy-done | bytes 536
  3.0 0.0 copy-start.7
  3.0 0.7 %copy-done.7 = bf16[16,8]{0,1:T(8,128)(2,1)S(1)} copy-done((bf16[16,8]{0,1:T(8,128)(2,1)S(1)}, bf16[16,8]{0,1:T(8,128)(2,1)}, u32[]{:S(2)}) %copy-start.7) | copy-done | bytes 280
  3.7 0.0 copy-start.8
  3.7 0.2 pack.1
  3.9 3.1 %collective-permute-start = (bf16[16,2176]{1,0:T(8,128)(2,1)S(1)}, bf16[16,2176]{1,0:T(8,128)(2,1)S(1)}, u32[]{:S(2)}, u32[]{:S(2)}) collective-permute-start(bf16[16,2176]{1,0:T(8,128)(2,1)S(1)} %pack.1), channel_id=1, source_target_pairs={{0,4},{1,5},{2,6},{3,7},{4,0},{5,1},{6,2},{7,3},{8,12},{9,13},{10,... | collective-permute-start | bytes 208904 | tf_op jit(solution)/shard_map/ppermute | solution.py:110
  7.0 2.6 %collective-permute-start.1 = (bf16[16,2176]{1,0:T(8,128)(2,1)S(1)}, bf16[16,2176]{1,0:T(8,128)(2,1)S(1)}, u32[]{:S(2)}, u32[]{:S(2)}) collective-permute-start(bf16[16,2176]{1,0:T(8,128)(2,1)S(1)} %pack.1), channel_id=1, source_target_pairs={{0,8},{1,9},{2,10},{3,11},{4,12},{5,13},{6,14},{7,15},{8,0},{9,1},... | collective-permute-start | bytes 208904 | tf_op jit(solution)/shard_map/ppermute | solution.py:110
  9.6 0.0 collective-permute-start.2
  9.6 0.0 collective-permute-done
  9.6 4.9 %collective-permute-done.1 = bf16[16,2176]{1,0:T(8,128)(2,1)S(1)} collective-permute-done((bf16[16,2176]{1,0:T(8,128)(2,1)S(1)}, bf16[16,2176]{1,0:T(8,128)(2,1)S(1)}, u32[]{:S(2)}, u32[]{:S(2)}) %collective-permute-start.1) | collective-permute-done | bytes 69664 | tf_op jit(solution)/shard_map/ppermute | solution.py:110
  14.5 1.3 %collective-permute-done.2 = bf16[16,2176]{1,0:T(8,128)(2,1)S(1)} collective-permute-done((bf16[16,2176]{1,0:T(8,128)(2,1)S(1)}, bf16[16,2176]{1,0:T(8,128)(2,1)S(1)}, u32[]{:S(2)}, u32[]{:S(2)}) %collective-permute-start.2) | collective-permute-done | bytes 69664 | tf_op jit(solution)/shard_map/ppermute | solution.py:110
  15.8 1.6 %collective-permute-start.3 = (bf16[64,2176]{1,0:T(8,128)(2,1)S(1)}, bf16[64,2176]{1,0:T(8,128)(2,1)S(1)}, u32[]{:S(2)}, u32[]{:S(2)}) collective-permute-start(bf16[64,2176]{1,0:T(8,128)(2,1)S(1)} %pad_maximum_fusion), channel_id=1, source_target_pairs={{0,2},{1,3},{2,0},{3,1},{4,6},{5,7},{6,4},{7,5},{8,10},{9,11},{10,... | collective-permute-start | bytes 835592 | tf_op jit(solution)/shard_map/ppermute | solution.py:110
  17.4 5.0 %collective-permute-done.3 = bf16[64,2176]{1,0:T(8,128)(2,1)S(1)} collective-permute-done((bf16[64,2176]{1,0:T(8,128)(2,1)S(1)}, bf16[64,2176]{1,0:T(8,128)(2,1)S(1)}, u32[]{:S(2)}, u32[]{:S(2)}) %collective-permute-start.3) | collective-permute-done | bytes 278560 | tf_op jit(solution)/shard_map/ppermute | solution.py:110
  22.5 0.1 collective-permute-start.4
  22.6 0.0 copy-done.9
  22.6 0.0 copy-done.8
  22.6 0.1 fusion.11
  22.7 1.8 %collective-permute-done.4.second_ref = bf16[128,2176]{1,0:T(8,128)(2,1)S(1)} collective-permute-done((bf16[128,2176]{1,0:T(8,128)(2,1)S(1)}, bf16[128,2176]{1,0:T(8,128)(2,1)S(1)}, u32[]{:S(2)}, u32[]{:S(2)}) %collective-permute-start.4) | collective-permute-done | bytes 557088 | tf_op jit(solution)/shard_map/ppermute | solution.py:110
  24.5 0.0 copy-start.1
  24.5 1.9 %copy-done.1 = bf16[1,2048,768]{2,1,0:T(8,128)(2,1)S(1)} copy-done((bf16[1,2048,768]{2,1,0:T(8,128)(2,1)S(1)}, bf16[1,2048,768]{2,1,0:T(8,128)(2,1)}, u32[]{:S(2)}) %copy-start.1) | copy-done | bytes 3145752
  26.4 0.0 copy-start.2
  26.4 1.9 %copy-done.2 = bf16[1,2048,768]{2,1,0:T(8,128)(2,1)S(1)} copy-done((bf16[1,2048,768]{2,1,0:T(8,128)(2,1)S(1)}, bf16[1,2048,768]{2,1,0:T(8,128)(2,1)}, u32[]{:S(2)}) %copy-start.2) | copy-done | bytes 3145752
  28.3 0.0 copy-start.3
  28.3 1.9 %copy-done.3 = bf16[1,768,2048]{2,1,0:T(8,128)(2,1)S(1)} copy-done((bf16[1,768,2048]{2,1,0:T(8,128)(2,1)S(1)}, bf16[1,768,2048]{2,1,0:T(8,128)(2,1)}, u32[]{:S(2)}) %copy-start.3) | copy-done | bytes 3145752
  30.2 0.0 copy-start.11
  30.2 4.5 %experts.1 = (f32[128,2048]{1,0:T(8,128)S(1)}, bf16[128,2048]{1,0:T(8,128)(2,1)S(1)}) custom-call(bf16[128,2176]{1,0:T(8,128)(2,1)S(1)} %constant_dynamic-update-slice_fusion.first_ref, bf16[128,2176]{1,0:T(8,128)(2,1)S(1)} %collective-permute-done.4.second_ref, bf16[1,2048,768]{2,1,0:T(8,128)(2,1)S(1)} %copy-done.1, bf16[1,2048,768]{2,1,0:T(8,128)(2,1)S(1)} %copy-done.2, ...), custom_call_target="tpu_custom_call" | custom-call | flops 2415919104 | bytes 11534336 | tf_op jit(solution)/shard_map/experts/pallas_call | solution.py:80
  34.7 0.2 collective-permute-start.5
  34.9 0.0 copy-done.11
  34.9 0.1 iota_compare_fusion
  35.0 0.0 copy-done
  35.0 0.7 %select_reduce_fusion = (f32[4,4,8]{2,1,0:T(4,128)S(1)}, f32[4,4,8,384]{3,2,1,0:T(8,128)S(1)}) fusion(pred[4,384]{1,0:T(4,128)(4,1)S(1)} %iota_compare_fusion, bf16[4,4,384,128]{3,2,1,0:T(8,128)(2,1)S(1)} %copy-done, bf16[1,4,32,128]{3,1,2,0:T(4,128)(2,1)S(1)} %bitcast.28), kind=kOutput, calls=%fused_computation.10 | convolution fusion | flops 12730240 | bytes 1804288 | tf_op jit(solution)/shard_map/bgqd,bgld->bgql/dot_general | solution.py:161
  35.7 0.9 %collective-permute-done.5 = bf16[128,2048]{1,0:T(8,128)(2,1)S(1)} collective-permute-done((bf16[128,2048]{1,0:T(8,128)(2,1)S(1)}, bf16[128,2048]{1,0:T(8,128)(2,1)S(1)}, u32[]{:S(2)}, u32[]{:S(2)}) %collective-permute-start.5) | collective-permute-done | bytes 524320 | tf_op jit(solution)/shard_map/ppermute | solution.py:110
  36.7 0.0 copy-start.10
  36.7 0.1 convert_add_fusion
  36.8 1.6 %collective-permute-start.6 = (bf16[64,2048]{1,0:T(8,128)(2,1)S(1)}, bf16[64,2048]{1,0:T(8,128)(2,1)S(1)}, u32[]{:S(2)}, u32[]{:S(2)}) collective-permute-start(bf16[64,2048]{1,0:T(8,128)(2,1)S(1)} %slice.45), channel_id=1, source_target_pairs={{0,2},{1,3},{2,0},{3,1},{4,6},{5,7},{6,4},{7,5},{8,10},{9,11},{10,... | collective-permute-start | bytes 786440 | tf_op jit(solution)/shard_map/ppermute | solution.py:110
  38.4 0.2 fusion.2
  38.6 0.0 copy-done.10
  38.6 0.0 copy-start.12
  38.7 6.6 %collective-permute-done.6 = bf16[64,2048]{1,0:T(8,128)(2,1)S(1)} collective-permute-done((bf16[64,2048]{1,0:T(8,128)(2,1)S(1)}, bf16[64,2048]{1,0:T(8,128)(2,1)S(1)}, u32[]{:S(2)}, u32[]{:S(2)}) %collective-permute-start.6) | collective-permute-done | bytes 262176 | tf_op jit(solution)/shard_map/ppermute | solution.py:110
  45.2 0.1 fusion.19
  45.3 0.0 copy-start.5
  45.3 1.1 %collective-permute-start.7 = (bf16[16,2048]{1,0:T(8,128)(2,1)S(1)}, bf16[16,2048]{1,0:T(8,128)(2,1)S(1)}, u32[]{:S(2)}, u32[]{:S(2)}) collective-permute-start(bf16[16,2048]{1,0:T(8,128)(2,1)S(1)} %get-tuple-element.8), channel_id=1, source_target_pairs={{0,4},{1,5},{2,6},{3,7},{4,0},{5,1},{6,2},{7,3},{8,12},{9,13},{10,... | collective-permute-start | bytes 196616 | tf_op jit(solution)/shard_map/ppermute | solution.py:110
  46.4 1.5 %collective-permute-start.8 = (bf16[16,2048]{1,0:T(8,128)(2,1)S(1)}, bf16[16,2048]{1,0:T(8,128)(2,1)S(1)}, u32[]{:S(2)}, u32[]{:S(2)}) collective-permute-start(bf16[16,2048]{1,0:T(8,128)(2,1)S(1)} %get-tuple-element.10), channel_id=1, source_target_pairs={{0,8},{1,9},{2,10},{3,11},{4,12},{5,13},{6,14},{7,15},{8,0},{9,1},... | collective-permute-start | bytes 196616 | tf_op jit(solution)/shard_map/ppermute | solution.py:110
  48.0 1.8 %collective-permute-start.9 = (bf16[16,2048]{1,0:T(8,128)(2,1)S(1)}, bf16[16,2048]{1,0:T(8,128)(2,1)S(1)}, u32[]{:S(2)}, u32[]{:S(2)}) collective-permute-start(bf16[16,2048]{1,0:T(8,128)(2,1)S(1)} %get-tuple-element.9), channel_id=1, source_target_pairs={{0,12},{1,13},{2,14},{3,15},{4,8},{5,9},{6,10},{7,11},{8,4},{9,5},... | collective-permute-start | bytes 196616 | tf_op jit(solution)/shard_map/ppermute | solution.py:110
  49.8 0.0 copy-done.12
  49.8 0.4 fusion.1
  50.2 0.7 %copy.30 = bf16[1,4,32,128]{3,1,2,0:T(4,128)(2,1)} copy(bf16[1,4,32,128]{3,2,1,0:T(8,128)(2,1)S(1)} %fusion.1) | data formatting | bytes 65536
  50.9 0.0 collective-permute-done.7
  50.9 3.3 %collective-permute-done.8 = bf16[16,2048]{1,0:T(8,128)(2,1)S(1)} collective-permute-done((bf16[16,2048]{1,0:T(8,128)(2,1)S(1)}, bf16[16,2048]{1,0:T(8,128)(2,1)S(1)}, u32[]{:S(2)}, u32[]{:S(2)}) %collective-permute-start.8) | collective-permute-done | bytes 65568 | tf_op jit(solution)/shard_map/ppermute | solution.py:110
  54.2 0.0 collective-permute-done.9
  54.2 0.0 copy-done.5
  54.2 0.7 %fusion.6 = bf16[16,2048]{1,0:T(8,128)(2,1)} fusion(f32[64,2048]{1,0:T(8,128)S(1)} %get-tuple-element.7, bf16[16,2048]{1,0:T(8,128)(2,1)S(1)} %collective-permute-done.9, bf16[16,2048]{1,0:T(8,128)(2,1)S(1)} %collective-permute-done.8, bf16[16,2048]{1,0:T(8,128)(2,1)S(1)} %collective-permute-done.7, bf16[16,2048]{1,0:T(8,128)(2,1)S(1)} %copy-done.5), kind=kLoop, calls=%fused_computation.16 | loop fusion | flops 294912 | bytes 458752 | tf_op jit(solution)/shard_map/convert_element_type | solution.py:127
  (12 shorter events, 0.2 us)
Async XLA Ops:
  0.6 34.4 %copy-start = (bf16[4,4,384,128]{3,2,1,0:T(8,128)(2,1)S(1)}, bf16[4,4,384,128]{3,2,1,0:T(8,128)(2,1)}, u32[]{:S(2)}) copy-start(bf16[4,4,384,128]{3,2,1,0:T(8,128)(2,1)} %param.21) | copy-start | bytes 4718596
  0.6 21.9 %copy-start.9 = (bf16[4,512]{1,0:T(4,128)(2,1)S(1)}, bf16[4,512]{1,0:T(4,128)(2,1)}, u32[]{:S(2)}) copy-start(bf16[4,512]{1,0:T(4,128)(2,1)} %param.23) | copy-start | bytes 12292
  1.5 0.8 %copy-start.4 = (bf16[16,2048]{1,0:T(8,128)(2,1)S(1)}, bf16[16,2048]{1,0:T(8,128)(2,1)}, u32[]{:S(2)}) copy-start(bf16[16,2048]{1,0:T(8,128)(2,1)} %hidden_ref.1) | copy-start | bytes 196612
  2.3 0.7 %copy-start.6 = (s32[16,8]{0,1:T(8,128)S(1)}, s32[16,8]{0,1:T(8,128)}, u32[]{:S(2)}) copy-start(s32[16,8]{0,1:T(8,128)} %param.15) | copy-start | bytes 1540
  3.0 0.7 %copy-start.7 = (bf16[16,8]{0,1:T(8,128)(2,1)S(1)}, bf16[16,8]{0,1:T(8,128)(2,1)}, u32[]{:S(2)}) copy-start(bf16[16,8]{0,1:T(8,128)(2,1)} %param.16) | copy-start | bytes 772
  3.7 18.9 %copy-start.8 = (bf16[4,4096]{1,0:T(4,128)(2,1)S(1)}, bf16[4,4096]{1,0:T(4,128)(2,1)}, u32[]{:S(2)}) copy-start(bf16[4,4096]{1,0:T(4,128)(2,1)} %param.20) | copy-start | bytes 98308
  3.9 5.7 %collective-permute-start = (bf16[16,2176]{1,0:T(8,128)(2,1)S(1)}, bf16[16,2176]{1,0:T(8,128)(2,1)S(1)}, u32[]{:S(2)}, u32[]{:S(2)}) collective-permute-start(bf16[16,2176]{1,0:T(8,128)(2,1)S(1)} %pack.1), channel_id=1, source_target_pairs={{0,4},{1,5},{2,6},{3,7},{4,0},{5,1},{6,2},{7,3},{8,12},{9,13},{10,... | collective-permute-start | bytes 208904 | tf_op jit(solution)/shard_map/ppermute | solution.py:110
  7.0 7.5 %collective-permute-start.1 = (bf16[16,2176]{1,0:T(8,128)(2,1)S(1)}, bf16[16,2176]{1,0:T(8,128)(2,1)S(1)}, u32[]{:S(2)}, u32[]{:S(2)}) collective-permute-start(bf16[16,2176]{1,0:T(8,128)(2,1)S(1)} %pack.1), channel_id=1, source_target_pairs={{0,8},{1,9},{2,10},{3,11},{4,12},{5,13},{6,14},{7,15},{8,0},{9,1},... | collective-permute-start | bytes 208904 | tf_op jit(solution)/shard_map/ppermute | solution.py:110
  9.6 6.2 %collective-permute-start.2 = (bf16[16,2176]{1,0:T(8,128)(2,1)S(1)}, bf16[16,2176]{1,0:T(8,128)(2,1)S(1)}, u32[]{:S(2)}, u32[]{:S(2)}) collective-permute-start(bf16[16,2176]{1,0:T(8,128)(2,1)S(1)} %pack.1), channel_id=1, source_target_pairs={{0,12},{1,13},{2,14},{3,15},{4,8},{5,9},{6,10},{7,11},{8,4},{9,5},... | collective-permute-start | bytes 208904 | tf_op jit(solution)/shard_map/ppermute | solution.py:110
  15.8 6.7 %collective-permute-start.3 = (bf16[64,2176]{1,0:T(8,128)(2,1)S(1)}, bf16[64,2176]{1,0:T(8,128)(2,1)S(1)}, u32[]{:S(2)}, u32[]{:S(2)}) collective-permute-start(bf16[64,2176]{1,0:T(8,128)(2,1)S(1)} %pad_maximum_fusion), channel_id=1, source_target_pairs={{0,2},{1,3},{2,0},{3,1},{4,6},{5,7},{6,4},{7,5},{8,10},{9,11},{10,... | collective-permute-start | bytes 835592 | tf_op jit(solution)/shard_map/ppermute | solution.py:110
  22.5 2.0 %collective-permute-start.4 = (bf16[128,2176]{1,0:T(8,128)(2,1)S(1)}, bf16[128,2176]{1,0:T(8,128)(2,1)S(1)}, u32[]{:S(2)}, u32[]{:S(2)}) collective-permute-start(bf16[128,2176]{1,0:T(8,128)(2,1)S(1)} %constant_dynamic-update-slice_fusion.first_ref), channel_id=1, source_target_pairs={{0,1},{1,0},{2,3},{3,2},{4,5},{5,4},{6,7},{7,6},{8,9},{9,8},{10,11... | collective-permute-start | bytes 1671176 | tf_op jit(solution)/shard_map/ppermute | solution.py:110
  24.5 1.9 %copy-start.1 = (bf16[1,2048,768]{2,1,0:T(8,128)(2,1)S(1)}, bf16[1,2048,768]{2,1,0:T(8,128)(2,1)}, u32[]{:S(2)}) copy-start(bf16[1,2048,768]{2,1,0:T(8,128)(2,1)} %gate_ref.1) | copy-start | bytes 9437188
  26.4 1.9 %copy-start.2 = (bf16[1,2048,768]{2,1,0:T(8,128)(2,1)S(1)}, bf16[1,2048,768]{2,1,0:T(8,128)(2,1)}, u32[]{:S(2)}) copy-start(bf16[1,2048,768]{2,1,0:T(8,128)(2,1)} %up_ref.1) | copy-start | bytes 9437188
  28.3 1.9 %copy-start.3 = (bf16[1,768,2048]{2,1,0:T(8,128)(2,1)S(1)}, bf16[1,768,2048]{2,1,0:T(8,128)(2,1)}, u32[]{:S(2)}) copy-start(bf16[1,768,2048]{2,1,0:T(8,128)(2,1)} %down_ref.1) | copy-start | bytes 9437188
  30.2 4.7 %copy-start.11 = (s32[4]{0:T(128)S(1)}, s32[4]{0:T(128)}, u32[]{:S(2)}) copy-start(s32[4]{0:T(128)} %param.25) | copy-start | bytes 52
  34.7 2.0 %collective-permute-start.5 = (bf16[128,2048]{1,0:T(8,128)(2,1)S(1)}, bf16[128,2048]{1,0:T(8,128)(2,1)S(1)}, u32[]{:S(2)}, u32[]{:S(2)}) collective-permute-start(bf16[128,2048]{1,0:T(8,128)(2,1)S(1)} %get-tuple-element.5), channel_id=1, source_target_pairs={{0,1},{1,0},{2,3},{3,2},{4,5},{5,4},{6,7},{7,6},{8,9},{9,8},{10,11... | collective-permute-start | bytes 1572872 | tf_op jit(solution)/shard_map/ppermute | solution.py:110
  36.7 1.9 %copy-start.10 = (bf16[4,512]{1,0:T(4,128)(2,1)S(1)}, bf16[4,512]{1,0:T(4,128)(2,1)}, u32[]{:S(2)}) copy-start(bf16[4,512]{1,0:T(4,128)(2,1)} %param.24) | copy-start | bytes 12292
  36.8 8.4 %collective-permute-start.6 = (bf16[64,2048]{1,0:T(8,128)(2,1)S(1)}, bf16[64,2048]{1,0:T(8,128)(2,1)S(1)}, u32[]{:S(2)}, u32[]{:S(2)}) collective-permute-start(bf16[64,2048]{1,0:T(8,128)(2,1)S(1)} %slice.45), channel_id=1, source_target_pairs={{0,2},{1,3},{2,0},{3,1},{4,6},{5,7},{6,4},{7,5},{8,10},{9,11},{10,... | collective-permute-start | bytes 786440 | tf_op jit(solution)/shard_map/ppermute | solution.py:110
  38.6 11.2 %copy-start.12 = (bf16[4,4,384,128]{3,2,1,0:T(8,128)(2,1)S(1)}, bf16[4,4,384,128]{3,2,1,0:T(8,128)(2,1)}, u32[]{:S(2)}) copy-start(bf16[4,4,384,128]{3,2,1,0:T(8,128)(2,1)} %param.22) | copy-start | bytes 4718596
  45.3 8.9 %copy-start.5 = (bf16[16,2048]{1,0:T(8,128)(2,1)S(1)}, bf16[16,2048]{1,0:T(8,128)(2,1)}, u32[]{:S(2)}) copy-start(bf16[16,2048]{1,0:T(8,128)(2,1)} %hidden_ref.1) | copy-start | bytes 196612
  45.3 5.5 %collective-permute-start.7 = (bf16[16,2048]{1,0:T(8,128)(2,1)S(1)}, bf16[16,2048]{1,0:T(8,128)(2,1)S(1)}, u32[]{:S(2)}, u32[]{:S(2)}) collective-permute-start(bf16[16,2048]{1,0:T(8,128)(2,1)S(1)} %get-tuple-element.8), channel_id=1, source_target_pairs={{0,4},{1,5},{2,6},{3,7},{4,0},{5,1},{6,2},{7,3},{8,12},{9,13},{10,... | collective-permute-start | bytes 196616 | tf_op jit(solution)/shard_map/ppermute | solution.py:110
  46.4 7.7 %collective-permute-start.8 = (bf16[16,2048]{1,0:T(8,128)(2,1)S(1)}, bf16[16,2048]{1,0:T(8,128)(2,1)S(1)}, u32[]{:S(2)}, u32[]{:S(2)}) collective-permute-start(bf16[16,2048]{1,0:T(8,128)(2,1)S(1)} %get-tuple-element.10), channel_id=1, source_target_pairs={{0,8},{1,9},{2,10},{3,11},{4,12},{5,13},{6,14},{7,15},{8,0},{9,1},... | collective-permute-start | bytes 196616 | tf_op jit(solution)/shard_map/ppermute | solution.py:110
  48.0 6.2 %collective-permute-start.9 = (bf16[16,2048]{1,0:T(8,128)(2,1)S(1)}, bf16[16,2048]{1,0:T(8,128)(2,1)S(1)}, u32[]{:S(2)}, u32[]{:S(2)}) collective-permute-start(bf16[16,2048]{1,0:T(8,128)(2,1)S(1)} %get-tuple-element.9), channel_id=1, source_target_pairs={{0,12},{1,13},{2,14},{3,15},{4,8},{5,9},{6,10},{7,11},{8,4},{9,5},... | collective-permute-start | bytes 196616 | tf_op jit(solution)/shard_map/ppermute | solution.py:110

commit v2 on v1

v2 whole, which is shorter than its diff:
```python
import functools
import jax
import jax.numpy as jnp
from jax import lax
from jax.experimental import pallas as pl
from jax.experimental.pallas import tpu as pltpu
from jax.sharding import PartitionSpec as P


EPS = 1e-06
LANES = 128
ANY = pl.BlockSpec(memory_space=pl.ANY)
VMEM = pl.BlockSpec(memory_space=pltpu.VMEM)


def in_hbm(array):
    return pltpu.with_memory_space_constraint(array, pltpu.HBM)


def pack_kernel(hidden_hbm, gain_hbm, ids_hbm, gates_hbm, packed_ref, hidden_ref, gain_ref, ids_ref, gates_ref, sems):
    copies = [
        pltpu.make_async_copy(source, target, sems.at[i])
        for i, (source, target) in enumerate(
            ((hidden_hbm, hidden_ref), (gain_hbm, gain_ref), (ids_hbm, ids_ref), (gates_hbm, gates_ref))
        )
    ]
    for copy in copies:
        copy.start()
    for copy in copies:
        copy.wait()
    rows, width = hidden_ref.shape
    lanes = packed_ref.shape[1] - width
    hidden = hidden_ref[...].astype(jnp.float32)
    scale = lax.rsqrt(jnp.mean(hidden * hidden, axis=-1, keepdims=True) + EPS)
    for j in range(width // LANES):
        span = slice(j * LANES, (j + 1) * LANES)
        gain = gain_ref[j : j + 1, :].astype(jnp.float32)
        packed_ref[:, span] = (hidden[:, span] * scale * gain).astype(jnp.bfloat16)
    expert = lax.broadcasted_iota(jnp.int32, (lanes, rows), 0)
    weight = jnp.zeros((lanes, rows), jnp.float32)
    for k in range(ids_ref.shape[0]):
        gate = gates_ref[k : k + 1, :].astype(jnp.float32)
        weight = weight + jnp.where(ids_ref[k : k + 1, :] == expert, gate, 0.0)
    row = lax.broadcasted_iota(jnp.int32, (rows, rows), 0)
    column = lax.broadcasted_iota(jnp.int32, (rows, rows), 1)
    packed_ref[:, width:] = lax.dot_general(
        (row == column).astype(jnp.bfloat16),
        weight.astype(jnp.bfloat16),
        (((1,), (1,)), ((), ())),
        preferred_element_type=jnp.float32,
    ).astype(jnp.bfloat16)


def pack(moe_input, norm_gain, route_ids, route_gates, experts):
    rows, width = moe_input.shape
    lanes = -(-experts // LANES) * LANES
    operands = (moe_input, norm_gain.reshape(width // LANES, LANES), route_ids.T, route_gates.T)
    return pl.pallas_call(
        pack_kernel,
        in_specs=[ANY] * 4,
        out_specs=VMEM,
        out_shape=pltpu.VMEM((rows, width + lanes), jnp.bfloat16),
        scratch_shapes=[pltpu.VMEM(a.shape, a.dtype) for a in operands] + [pltpu.SemaphoreType.DMA((4,))],
        name="pack",
        compiler_params=pltpu.CompilerParams(vmem_limit_bytes=2 << 20),
        cost_estimate=pl.CostEstimate(flops=rows * width * 8, bytes_accessed=rows * width * 4, transcendentals=rows),
    )(*map(in_hbm, operands))


def load_kernel(pieces, count, *refs):
    sources, targets, sems = refs[:count], refs[-1 - count : -1], refs[-1]
    copies = []
    for i, (source, target) in enumerate(zip(sources, targets)):
        size = source.shape[1] // pieces
        for j in range(pieces):
            span = pl.ds(j * size, size)
            copies.append(
                pltpu.make_async_copy(source.at[0, span, :], target.at[span, :], sems.at[i * pieces + j])
            )
    for copy in copies:
        copy.start()
    for copy in copies:
        copy.wait()


def load_weights(weights, after):
    pieces = 4
    count = len(weights)
    size = sum(w.size for w in weights)
    return pl.pallas_call(
        functools.partial(load_kernel, pieces, count),
        in_specs=[ANY] * (count + len(after)),
        out_specs=[VMEM] * count,
        out_shape=[pltpu.VMEM(w.shape[1:], w.dtype) for w in weights],
        scratch_shapes=[pltpu.SemaphoreType.DMA((pieces * count,))],
        name="load",
        compiler_params=pltpu.CompilerParams(vmem_limit_bytes=1 << 20),
        cost_estimate=pl.CostEstimate(flops=200 * size, bytes_accessed=2 * size, transcendentals=0),
    )(*map(in_hbm, weights), *after)


def expert_kernel(first_ref, second_ref, gate_ref, up_ref, down_ref, kept_ref, sent_ref, active_ref):
    width, hidden = gate_ref.shape
    half = first_ref.shape[0]
    tile = 256 if hidden % 256 == 0 else hidden
    rows = jnp.concatenate([first_ref[:, :width], second_ref[:, :width]], axis=0)
    for j in range(0, hidden, tile):
        gate_part = jnp.dot(rows, gate_ref[:, j : j + tile], preferred_element_type=jnp.float32)
        up_part = jnp.dot(rows, up_ref[:, j : j + tile], preferred_element_type=jnp.float32)
        active = gate_part / (1.0 + jnp.exp(-gate_part)) * up_part
        active_ref[:, j : j + tile] = active.astype(jnp.bfloat16)
    expert = lax.axis_index("req")
    packed = jnp.concatenate([first_ref[:, width:], second_ref[:, width:]], axis=0).astype(jnp.float32)
    mine = lax.broadcasted_iota(jnp.int32, packed.shape, 1) == expert
    weight = jnp.sum(jnp.where(mine, packed, 0.0), axis=1, keepdims=True)
    tile = 512 if width % 512 == 0 else width
    for j in range(0, width, tile):
        produced = jnp.dot(active_ref[...], down_ref[:, j : j + tile], preferred_element_type=jnp.float32)
        produced = produced.astype(jnp.bfloat16).astype(jnp.float32) * weight
        kept_ref[:, j : j + tile] = produced[:half]
        sent_ref[:, j : j + tile] = produced[half:].astype(jnp.bfloat16)


def expert_section(first, second, w_gate, w_up, w_down):
    half, _ = first.shape
    width, hidden = w_gate.shape
    return pl.pallas_call(
        expert_kernel,
        in_specs=[VMEM] * 5,
        out_specs=[VMEM] * 2,
        out_shape=[
            pltpu.VMEM((half, width), jnp.float32),
            pltpu.VMEM((half, width), jnp.bfloat16),
        ],
        scratch_shapes=[pltpu.VMEM((2 * half, hidden), jnp.bfloat16)],
        name="experts",
        compiler_params=pltpu.CompilerParams(vmem_limit_bytes=8 << 20),
        cost_estimate=pl.CostEstimate(
            flops=12 * half * width * hidden,
            bytes_accessed=6 * width * hidden + 8 * half * width,
            transcendentals=2 * half * hidden,
        ),
    )(first, second, w_gate, w_up, w_down)


def attend_kernel(queries_hbm, keys_hbm, values_hbm, new_keys_hbm, new_values_hbm, lengths_ref, out_ref,
                  queries_ref, keys_ref, values_ref, new_keys_ref, new_values_ref, small_sems, sems):
    batch, heads, span, size = keys_ref.shape
    group = queries_ref.shape[1] // (heads * size)
    small = [
        pltpu.make_async_copy(source, target, small_sems.at[i])
        for i, (source, target) in enumerate(
            ((queries_hbm, queries_ref), (new_keys_hbm, new_keys_ref), (new_values_hbm, new_values_ref))
        )
    ]
    large = []
    for b in range(batch):
        large.append(pltpu.make_async_copy(keys_hbm.at[b], keys_ref.at[b], sems.at[2 * b]))
        large.append(pltpu.make_async_copy(values_hbm.at[b], values_ref.at[b], sems.at[2 * b + 1]))
    for copy in small + large:
        copy.start()
    for copy in small:
        copy.wait()
    queries = queries_ref[...].astype(jnp.float32)
    new_keys = new_keys_ref[...].astype(jnp.float32)
    new_values = new_values_ref[...].astype(jnp.float32)
    position = lax.broadcasted_iota(jnp.int32, (group, span), 1)
    for b in range(batch):
        large[2 * b].wait()
        live = position < lengths_ref[b]
        probs = []
        for h in range(heads):
            first = h * group
            query = jnp.concatenate(
                [queries[b : b + 1, (first + i) * size : (first + i + 1) * size] for i in range(group)], axis=0
            )
            scores = lax.dot_general(
                query.astype(jnp.bfloat16),
                keys_ref[b, h],
                (((1,), (1,)), ((), ())),
                preferred_element_type=jnp.float32,
            ) * (size ** -0.5)
            own = jnp.sum(query * new_keys[b : b + 1, h * size : (h + 1) * size], axis=1, keepdims=True)
            own = own * (size ** -0.5)
            highest = jnp.maximum(jnp.max(jnp.where(live, scores, -jnp.inf), axis=1, keepdims=True), own)
            weights = jnp.where(live, jnp.exp(scores - highest), 0.0)
            own_weight = jnp.exp(own - highest)
            totals = jnp.sum(weights, axis=1, keepdims=True) + own_weight
            probs.append(((weights / totals).astype(jnp.bfloat16), (own_weight / totals).astype(jnp.bfloat16)))
        large[2 * b + 1].wait()
        for h, (prob, own_prob) in enumerate(probs):
            mixed = jnp.dot(prob, values_ref[b, h], preferred_element_type=jnp.float32)
            mixed = mixed + own_prob.astype(jnp.float32) * new_values[b : b + 1, h * size : (h + 1) * size]
            mixed = mixed.astype(out_ref.dtype)
            for i in range(group):
                column = (h * group + i) * size
                out_ref[b : b + 1, column : column + size] = mixed[i : i + 1]


def attend(queries, keys_cache, values_cache, new_keys, new_values, cache_lengths):
    operands = (queries, keys_cache, values_cache, new_keys, new_values)
    batch, _, span, size = keys_cache.shape
    return pl.pallas_call(
        attend_kernel,
        in_specs=[ANY] * 5 + [pl.BlockSpec(memory_space=pltpu.SMEM)],
        out_specs=VMEM,
        out_shape=jax.ShapeDtypeStruct(queries.shape, queries.dtype),
        scratch_shapes=[pltpu.VMEM(a.shape, a.dtype) for a in operands]
        + [pltpu.SemaphoreType.DMA((3,)), pltpu.SemaphoreType.DMA((2 * batch,))],
        name="attend",
        compiler_params=pltpu.CompilerParams(vmem_limit_bytes=12 << 20),
        cost_estimate=pl.CostEstimate(
            flops=200 * keys_cache.size, bytes_accessed=4 * keys_cache.size, transcendentals=queries.size * span // size
        ),
    )(*map(in_hbm, operands), cache_lengths)


def exchange(value, distance, devices):
    return lax.ppermute(value, "req", [(i, i ^ distance) for i in range(devices)])


def gathered_layer(packed, w_gate, w_up, w_down, hidden, devices):
    rows, _ = hidden.shape
    far = range(4, devices, 4)
    column = jnp.concatenate([packed] + [exchange(packed, k, devices) for k in far], axis=0)
    weights = load_weights((w_gate, w_up, w_down), ())
    plane = jnp.concatenate([column, exchange(column, 2, devices)], axis=0)
    other = exchange(plane, 1, devices)
    kept, sent = expert_section(plane, other, *weights)
    kept = kept + exchange(sent, 1, devices).astype(jnp.float32)
    half = kept.shape[0] // 2
    kept = kept[:half] + exchange(kept[half:].astype(jnp.bfloat16), 2, devices).astype(jnp.float32)
    total = hidden.astype(jnp.float32) + kept[:rows]
    for i, k in enumerate(far):
        block = kept[(i + 1) * rows : (i + 2) * rows].astype(jnp.bfloat16)
        total = total + exchange(block, k, devices).astype(jnp.float32)
    return total.astype(jnp.bfloat16)


def slot_table(route_ids, experts, capacity):
    onehot = (route_ids[:, :, None] == jnp.arange(experts, dtype=jnp.int32)[None, None, :]).astype(
        jnp.float32
    )
    present = jnp.sum(onehot, axis=1)
    earlier = jnp.cumsum(present, axis=0) - present
    levels = jnp.arange(capacity, dtype=jnp.float32)
    placed = present[:, :, None] * (earlier[:, :, None] == levels[None, None, :]).astype(
        jnp.float32
    )
    return (onehot, placed)


def expert_apply(received, w_gate, w_up, w_down):
    gate_part = jnp.einsum("nesd,edf->nesf", received, w_gate, preferred_element_type=jnp.float32)
    up_part = jnp.einsum("nesd,edf->nesf", received, w_up, preferred_element_type=jnp.float32)
    active = (jax.nn.silu(gate_part) * up_part).astype(jnp.bfloat16)
    return jnp.einsum("nesf,efd->nesd", active, w_down, preferred_element_type=jnp.float32).astype(
        jnp.bfloat16
    )


def slotted_layer(
    moe_input, norm_gain, route_ids, route_gates, expert_gate, expert_up, expert_down, capacity
):
    row_count = moe_input.shape[0]
    model_width = moe_input.shape[1]
    local_experts = expert_gate.shape[0]
    devices = lax.axis_size("req")
    experts = devices * local_experts
    hidden = moe_input.astype(jnp.float32)
    normed = (
        hidden
        * lax.rsqrt(jnp.mean(hidden * hidden, axis=-1, keepdims=True) + EPS)
        * norm_gain.astype(jnp.float32)
    ).astype(jnp.bfloat16)
    onehot, placed = slot_table(route_ids, experts, capacity)
    selector = placed.reshape(row_count, experts * capacity).astype(jnp.bfloat16)
    outgoing = jnp.einsum("rs,rd->sd", selector, normed, preferred_element_type=jnp.float32).astype(
        jnp.bfloat16
    )
    outgoing = outgoing.reshape(devices, local_experts, capacity, model_width)
    produced = expert_apply(
        lax.all_to_all(outgoing, "req", split_axis=0, concat_axis=0, tiled=True),
        expert_gate,
        expert_up,
        expert_down,
    )
    returned = lax.all_to_all(produced, "req", split_axis=0, concat_axis=0, tiled=True)
    weight = jnp.einsum("rke,rk->re", onehot, route_gates.astype(jnp.float32))
    combine = (
        (weight[:, :, None] * placed).reshape(row_count, experts * capacity).astype(jnp.bfloat16)
    )
    expert_sum = jnp.dot(
        combine,
        returned.reshape(experts * capacity, model_width),
        preferred_element_type=jnp.float32,
    )
    moe_out = (hidden + expert_sum).astype(jnp.bfloat16)
    return moe_out


def layer(
    moe_input,
    norm_gain,
    route_ids,
    route_gates,
    expert_gate,
    expert_up,
    expert_down,
    queries,
    keys_cache,
    values_cache,
    new_keys,
    new_values,
    cache_lengths,
):
    row_count = moe_input.shape[0]
    local_experts = expert_gate.shape[0]
    devices = lax.axis_size("req")
    experts = devices * local_experts
    capacity = min(row_count, max(2, 16 * row_count // experts))
    if local_experts == 1 and capacity == row_count and devices >= 8 and devices & (devices - 1) == 0:
        packed = pack(moe_input, norm_gain, route_ids, route_gates, experts)
        moe_out = gathered_layer(packed, expert_gate, expert_up, expert_down, moe_input, devices)
    else:
        moe_out = slotted_layer(
            moe_input, norm_gain, route_ids, route_gates, expert_gate, expert_up, expert_down, capacity
        )
    attention_out = attend(queries, keys_cache, values_cache, new_keys, new_values, cache_lengths)
    return (moe_out, attention_out)


def solution(mesh):
    in_specs = (
        P(("grp", "req"), None),
        P(),
        P(("grp", "req"), None),
        P(("grp", "req"), None),
        P("req", None, None),
        P("req", None, None),
        P("req", None, None),
        P(("grp", "req"), None),
        P(("grp", "req"), None, None, None),
        P(("grp", "req"), None, None, None),
        P(("grp", "req"), None),
        P(("grp", "req"), None),
        P(("grp", "req")),
    )
    out_specs = (P(("grp", "req"), None), P(("grp", "req"), None))
    return jax.shard_map(layer, mesh=mesh, in_specs=in_specs, out_specs=out_specs, check_vma=False)
```

time: 55.2 us -> 48.6 us (0.88)
  local copies, waits for them, and re-layouts: 9.52 us -> 0.12 us
  Pallas kernels: 4.67 us -> 12.8 us
  waiting for transfers between devices: 23.8 us -> 19.8 us
  matrix products: 1.28 us -> 0 us
    unnamed x31 -> x8, local copies, waits for them, and re-layouts: 8.61 us -> 0.05 us
    pallas_call x2 -> x4, Pallas kernels: 4.67 us -> 12.8 us  [the longest x1 5.34 us: attend(): pl.pallas_call(attend_kernel, in_specs=[ANY] * 5 + [pl.BlockSpec(memory_s...]
    ppermute x10, waiting for transfers between devices: 23.8 us -> 19.8 us  [exchange(): lax.ppermute(value, 'req', [(i, i ^ distance) for i in range(devices)])]
    dot_general x3 -> x0, matrix products: 1.28 us -> none  [the longest x1 0.73 us: attend(): jnp.einsum('bgqd,bgld->bgql', grouped, keys_cache, preferred_element_type...]
    reshape x2 -> x0, local copies, waits for them, and re-layouts: 0.83 us -> none  [the longest x1 0.82 us: pack(): norm_gain.reshape(1, width)]
  transfers between devices with their start and end apart: 10 -> 10, of which waited for: 7 -> 5; matrix products, arithmetic and copies ran while one was open for 4% -> 0% of each run, Pallas kernels for 0% -> 19%
where the time goes in v2:
time: 48.6 us; the launch traced here: 48.4 us
  waiting for transfers between devices  19.8 us (41%)
  starting transfers between devices  14 us (29%)
  Pallas kernels  12.8 us (26%)
  other arithmetic  0.9 us (2%)
  between operations  0.78 us (2%)
    ppermute x10, waiting for transfers between devices, exchange(): lax.ppermute(value, 'req', [(i, i ^ distance) for i in range(devices)])  19.8 us
    ppermute x10, starting transfers between devices, exchange(): lax.ppermute(value, 'req', [(i, i ^ distance) for i in range(devices)])  14 us
    pallas_call x1, Pallas kernels, attend(): pl.pallas_call(attend_kernel, in_specs=[ANY] * 5 + [pl.BlockSpec(memory_s...  5.34 us
    pallas_call x1, Pallas kernels, load_weights(): pl.pallas_call(functools.partial(load_kernel, pieces, count), in_specs=[A...  3.8 us
    pallas_call x1, Pallas kernels, expert_section(): pl.pallas_call(expert_kernel, in_specs=[VMEM] * 5, out_specs=[VMEM] * 2,...  2.63 us
    pallas_call x1, Pallas kernels, pack(): pl.pallas_call(pack_kernel, in_specs=[ANY] * 4, out_specs=VMEM, out_shape...  1.06 us
  transfers between devices with their start and end apart: 10, of which 5 were waited for; matrix products, arithmetic and copies ran while one was open for 0% of the time, Pallas kernels for 19%

profile of v2, /device:TPU:0, one launch (start us, length us, event | category | flops | bytes accessed | tf_op | source)
XLA Modules:
  0.0 48.4 jit_solution(13817768028342136512)
XLA Ops:
  0.6 1.1 %pack.1 = bf16[16,2176]{1,0:T(8,128)(2,1)S(1)} custom-call(bf16[16,2048]{1,0:T(8,128)(2,1)} %hidden_hbm.1, bf16[16,128]{1,0:T(8,128)(2,1)} %bitcast.3, s32[8,16]{1,0:T(8,128)} %bitcast.4, bf16[8,16]{1,0:T(8,128)(2,1)} %bitcast.5), custom_call_target="tpu_custom_call" | custom-call | flops 262144 | bytes 131072 | tf_op jit(solution)/shard_map/pack/pallas_call | solution.py:58
  1.7 3.1 %collective-permute-start = (bf16[16,2176]{1,0:T(8,128)(2,1)S(1)}, bf16[16,2176]{1,0:T(8,128)(2,1)S(1)}, u32[]{:S(2)}, u32[]{:S(2)}) collective-permute-start(bf16[16,2176]{1,0:T(8,128)(2,1)S(1)} %pack.1), channel_id=1, source_target_pairs={{0,4},{1,5},{2,6},{3,7},{4,0},{5,1},{6,2},{7,3},{8,12},{9,13},{10,... | collective-permute-start | bytes 208904 | tf_op jit(solution)/shard_map/ppermute | solution.py:219
  4.8 2.6 %collective-permute-start.1 = (bf16[16,2176]{1,0:T(8,128)(2,1)S(1)}, bf16[16,2176]{1,0:T(8,128)(2,1)S(1)}, u32[]{:S(2)}, u32[]{:S(2)}) collective-permute-start(bf16[16,2176]{1,0:T(8,128)(2,1)S(1)} %pack.1), channel_id=1, source_target_pairs={{0,8},{1,9},{2,10},{3,11},{4,12},{5,13},{6,14},{7,15},{8,0},{9,1},... | collective-permute-start | bytes 208904 | tf_op jit(solution)/shard_map/ppermute | solution.py:219
  7.4 0.0 collective-permute-start.2
  7.4 0.0 collective-permute-done
  7.4 4.9 %collective-permute-done.1 = bf16[16,2176]{1,0:T(8,128)(2,1)S(1)} collective-permute-done((bf16[16,2176]{1,0:T(8,128)(2,1)S(1)}, bf16[16,2176]{1,0:T(8,128)(2,1)S(1)}, u32[]{:S(2)}, u32[]{:S(2)}) %collective-permute-start.1) | collective-permute-done | bytes 69664 | tf_op jit(solution)/shard_map/ppermute | solution.py:219
  12.3 1.3 %collective-permute-done.2 = bf16[16,2176]{1,0:T(8,128)(2,1)S(1)} collective-permute-done((bf16[16,2176]{1,0:T(8,128)(2,1)S(1)}, bf16[16,2176]{1,0:T(8,128)(2,1)S(1)}, u32[]{:S(2)}, u32[]{:S(2)}) %collective-permute-start.2) | collective-permute-done | bytes 69664 | tf_op jit(solution)/shard_map/ppermute | solution.py:219
  13.6 1.6 %collective-permute-start.3 = (bf16[64,2176]{1,0:T(8,128)(2,1)S(1)}, bf16[64,2176]{1,0:T(8,128)(2,1)S(1)}, u32[]{:S(2)}, u32[]{:S(2)}) collective-permute-start(bf16[64,2176]{1,0:T(8,128)(2,1)S(1)} %pad_maximum_fusion), channel_id=1, source_target_pairs={{0,2},{1,3},{2,0},{3,1},{4,6},{5,7},{6,4},{7,5},{8,10},{9,11},{10,... | collective-permute-start | bytes 835592 | tf_op jit(solution)/shard_map/ppermute | solution.py:219
  15.3 5.0 %collective-permute-done.3 = bf16[64,2176]{1,0:T(8,128)(2,1)S(1)} collective-permute-done((bf16[64,2176]{1,0:T(8,128)(2,1)S(1)}, bf16[64,2176]{1,0:T(8,128)(2,1)S(1)}, u32[]{:S(2)}, u32[]{:S(2)}) %collective-permute-start.3) | collective-permute-done | bytes 278560 | tf_op jit(solution)/shard_map/ppermute | solution.py:219
  20.3 0.1 collective-permute-start.4
  20.4 3.8 %load.1 = (bf16[2048,768]{1,0:T(8,128)(2,1)S(1)}, bf16[2048,768]{1,0:T(8,128)(2,1)S(1)}, bf16[768,2048]{1,0:T(8,128)(2,1)S(1)}) custom-call(bf16[1,2048,768]{2,1,0:T(8,128)(2,1)} %refs_0_.1, bf16[1,2048,768]{2,1,0:T(8,128)(2,1)} %refs_1_.1, bf16[1,768,2048]{2,1,0:T(8,128)(2,1)} %refs_2_.1), custom_call_target="tpu_custom_call" | custom-call | flops 943718400 | bytes 9437184 | tf_op jit(solution)/shard_map/load/pallas_call | solution.py:90
  24.2 0.0 collective-permute-done.4.second_ref
  24.2 2.6 %experts.1 = (f32[128,2048]{1,0:T(8,128)S(1)}, bf16[128,2048]{1,0:T(8,128)(2,1)S(1)}) custom-call(bf16[128,2176]{1,0:T(8,128)(2,1)S(1)} %constant_dynamic-update-slice_fusion.first_ref, bf16[128,2176]{1,0:T(8,128)(2,1)S(1)} %collective-permute-done.4.second_ref, bf16[2048,768]{1,0:T(8,128)(2,1)S(1)} %get-tuple-element.7.gate_ref, ...), custom_call_target="tpu_custom_call" | custom-call | flops 2415919104 | bytes 11534336 | tf_op jit(solution)/shard_map/experts/pallas_call | solution.py:127
  26.9 0.0 copy-start
  26.9 0.6 %collective-permute-start.5 = (bf16[128,2048]{1,0:T(8,128)(2,1)S(1)}, bf16[128,2048]{1,0:T(8,128)(2,1)S(1)}, u32[]{:S(2)}, u32[]{:S(2)}) collective-permute-start(bf16[128,2048]{1,0:T(8,128)(2,1)S(1)} %get-tuple-element.11), channel_id=1, source_target_pairs={{0,1},{1,0},{2,3},{3,2},{4,5},{5,4},{6,7},{7,6},{8,9},{9,8},{10,11... | collective-permute-start | bytes 1572872 | tf_op jit(solution)/shard_map/ppermute | solution.py:219
  27.4 1.5 %collective-permute-done.5 = bf16[128,2048]{1,0:T(8,128)(2,1)S(1)} collective-permute-done((bf16[128,2048]{1,0:T(8,128)(2,1)S(1)}, bf16[128,2048]{1,0:T(8,128)(2,1)S(1)}, u32[]{:S(2)}, u32[]{:S(2)}) %collective-permute-start.5) | collective-permute-done | bytes 524320 | tf_op jit(solution)/shard_map/ppermute | solution.py:219
  29.0 0.1 convert_add_fusion
  29.1 0.0 copy-start.1
  29.1 1.6 %collective-permute-start.6 = (bf16[64,2048]{1,0:T(8,128)(2,1)S(1)}, bf16[64,2048]{1,0:T(8,128)(2,1)S(1)}, u32[]{:S(2)}, u32[]{:S(2)}) collective-permute-start(bf16[64,2048]{1,0:T(8,128)(2,1)S(1)} %slice.45), channel_id=1, source_target_pairs={{0,2},{1,3},{2,0},{3,1},{4,6},{5,7},{6,4},{7,5},{8,10},{9,11},{10,... | collective-permute-start | bytes 786440 | tf_op jit(solution)/shard_map/ppermute | solution.py:219
  30.7 7.1 %collective-permute-done.6 = bf16[64,2048]{1,0:T(8,128)(2,1)S(1)} collective-permute-done((bf16[64,2048]{1,0:T(8,128)(2,1)S(1)}, bf16[64,2048]{1,0:T(8,128)(2,1)S(1)}, u32[]{:S(2)}, u32[]{:S(2)}) %collective-permute-start.6) | collective-permute-done | bytes 262176 | tf_op jit(solution)/shard_map/ppermute | solution.py:219
  37.8 0.1 fusion.4
  37.9 1.1 %collective-permute-start.7 = (bf16[16,2048]{1,0:T(8,128)(2,1)S(1)}, bf16[16,2048]{1,0:T(8,128)(2,1)S(1)}, u32[]{:S(2)}, u32[]{:S(2)}) collective-permute-start(bf16[16,2048]{1,0:T(8,128)(2,1)S(1)} %get-tuple-element.14), channel_id=1, source_target_pairs={{0,4},{1,5},{2,6},{3,7},{4,0},{5,1},{6,2},{7,3},{8,12},{9,13},{10,... | collective-permute-start | bytes 196616 | tf_op jit(solution)/shard_map/ppermute | solution.py:219
  39.0 1.5 %collective-permute-start.8 = (bf16[16,2048]{1,0:T(8,128)(2,1)S(1)}, bf16[16,2048]{1,0:T(8,128)(2,1)S(1)}, u32[]{:S(2)}, u32[]{:S(2)}) collective-permute-start(bf16[16,2048]{1,0:T(8,128)(2,1)S(1)} %get-tuple-element.16), channel_id=1, source_target_pairs={{0,8},{1,9},{2,10},{3,11},{4,12},{5,13},{6,14},{7,15},{8,0},{9,1},... | collective-permute-start | bytes 196616 | tf_op jit(solution)/shard_map/ppermute | solution.py:219
  40.5 1.8 %collective-permute-start.9 = (bf16[16,2048]{1,0:T(8,128)(2,1)S(1)}, bf16[16,2048]{1,0:T(8,128)(2,1)S(1)}, u32[]{:S(2)}, u32[]{:S(2)}) collective-permute-start(bf16[16,2048]{1,0:T(8,128)(2,1)S(1)} %get-tuple-element.15), channel_id=1, source_target_pairs={{0,12},{1,13},{2,14},{3,15},{4,8},{5,9},{6,10},{7,11},{8,4},{9,5},... | collective-permute-start | bytes 196616 | tf_op jit(solution)/shard_map/ppermute | solution.py:219
  42.4 0.0 copy-done
  42.4 5.3 %attend.1 = bf16[4,4096]{1,0:T(4,128)(2,1)} custom-call(bf16[4,4096]{1,0:T(4,128)(2,1)} %queries_hbm.1, bf16[4,4,384,128]{3,2,1,0:T(8,128)(2,1)} %keys_hbm.1, bf16[4,4,384,128]{3,2,1,0:T(8,128)(2,1)} %values_hbm.1, bf16[4,512]{1,0:T(4,128)(2,1)} %new_keys_hbm.1, bf16[4,512]{1,0:T(4,128)(2,1)} %new_values_hbm.1, s32[4]{0:T(128)S(1)} %copy-done), custom_call_target="tpu_custom_call" | custom-call | flops 157286400 | bytes 3145728 | tf_op jit(solution)/shard_map/attend/pallas_call | solution.py:203
  47.7 0.0 collective-permute-done.7
  47.7 0.0 collective-permute-done.8
  47.7 0.0 collective-permute-done.9
  47.7 0.0 copy-done.1
  47.7 0.7 %fusion.3 = bf16[16,2048]{1,0:T(8,128)(2,1)} fusion(f32[64,2048]{1,0:T(8,128)S(1)} %get-tuple-element.13, bf16[16,2048]{1,0:T(8,128)(2,1)S(1)} %collective-permute-done.9, bf16[16,2048]{1,0:T(8,128)(2,1)S(1)} %collective-permute-done.8, bf16[16,2048]{1,0:T(8,128)(2,1)S(1)} %collective-permute-done.7, bf16[16,2048]{1,0:T(8,128)(2,1)S(1)} %copy-done.1), kind=kLoop, calls=%fused_computation.8 | loop fusion | flops 294912 | bytes 458752 | tf_op jit(solution)/shard_map/convert_element_type | solution.py:237
  (8 shorter events, 0.1 us)
Async XLA Ops:
  1.7 5.7 %collective-permute-start = (bf16[16,2176]{1,0:T(8,128)(2,1)S(1)}, bf16[16,2176]{1,0:T(8,128)(2,1)S(1)}, u32[]{:S(2)}, u32[]{:S(2)}) collective-permute-start(bf16[16,2176]{1,0:T(8,128)(2,1)S(1)} %pack.1), channel_id=1, source_target_pairs={{0,4},{1,5},{2,6},{3,7},{4,0},{5,1},{6,2},{7,3},{8,12},{9,13},{10,... | collective-permute-start | bytes 208904 | tf_op jit(solution)/shard_map/ppermute | solution.py:219
  4.8 7.5 %collective-permute-start.1 = (bf16[16,2176]{1,0:T(8,128)(2,1)S(1)}, bf16[16,2176]{1,0:T(8,128)(2,1)S(1)}, u32[]{:S(2)}, u32[]{:S(2)}) collective-permute-start(bf16[16,2176]{1,0:T(8,128)(2,1)S(1)} %pack.1), channel_id=1, source_target_pairs={{0,8},{1,9},{2,10},{3,11},{4,12},{5,13},{6,14},{7,15},{8,0},{9,1},... | collective-permute-start | bytes 208904 | tf_op jit(solution)/shard_map/ppermute | solution.py:219
  7.4 6.2 %collective-permute-start.2 = (bf16[16,2176]{1,0:T(8,128)(2,1)S(1)}, bf16[16,2176]{1,0:T(8,128)(2,1)S(1)}, u32[]{:S(2)}, u32[]{:S(2)}) collective-permute-start(bf16[16,2176]{1,0:T(8,128)(2,1)S(1)} %pack.1), channel_id=1, source_target_pairs={{0,12},{1,13},{2,14},{3,15},{4,8},{5,9},{6,10},{7,11},{8,4},{9,5},... | collective-permute-start | bytes 208904 | tf_op jit(solution)/shard_map/ppermute | solution.py:219
  13.6 6.7 %collective-permute-start.3 = (bf16[64,2176]{1,0:T(8,128)(2,1)S(1)}, bf16[64,2176]{1,0:T(8,128)(2,1)S(1)}, u32[]{:S(2)}, u32[]{:S(2)}) collective-permute-start(bf16[64,2176]{1,0:T(8,128)(2,1)S(1)} %pad_maximum_fusion), channel_id=1, source_target_pairs={{0,2},{1,3},{2,0},{3,1},{4,6},{5,7},{6,4},{7,5},{8,10},{9,11},{10,... | collective-permute-start | bytes 835592 | tf_op jit(solution)/shard_map/ppermute | solution.py:219
  20.3 3.9 %collective-permute-start.4 = (bf16[128,2176]{1,0:T(8,128)(2,1)S(1)}, bf16[128,2176]{1,0:T(8,128)(2,1)S(1)}, u32[]{:S(2)}, u32[]{:S(2)}) collective-permute-start(bf16[128,2176]{1,0:T(8,128)(2,1)S(1)} %constant_dynamic-update-slice_fusion.first_ref), channel_id=1, source_target_pairs={{0,1},{1,0},{2,3},{3,2},{4,5},{5,4},{6,7},{7,6},{8,9},{9,8},{10,11... | collective-permute-start | bytes 1671176 | tf_op jit(solution)/shard_map/ppermute | solution.py:219
  26.9 15.5 %copy-start = (s32[4]{0:T(128)S(1)}, s32[4]{0:T(128)}, u32[]{:S(2)}) copy-start(s32[4]{0:T(128)} %lengths_ref.1) | copy-start | bytes 52
  26.9 2.1 %collective-permute-start.5 = (bf16[128,2048]{1,0:T(8,128)(2,1)S(1)}, bf16[128,2048]{1,0:T(8,128)(2,1)S(1)}, u32[]{:S(2)}, u32[]{:S(2)}) collective-permute-start(bf16[128,2048]{1,0:T(8,128)(2,1)S(1)} %get-tuple-element.11), channel_id=1, source_target_pairs={{0,1},{1,0},{2,3},{3,2},{4,5},{5,4},{6,7},{7,6},{8,9},{9,8},{10,11... | collective-permute-start | bytes 1572872 | tf_op jit(solution)/shard_map/ppermute | solution.py:219
  29.1 18.6 %copy-start.1 = (bf16[16,2048]{1,0:T(8,128)(2,1)S(1)}, bf16[16,2048]{1,0:T(8,128)(2,1)}, u32[]{:S(2)}) copy-start(bf16[16,2048]{1,0:T(8,128)(2,1)} %hidden_hbm.1) | copy-start | bytes 196612
  29.1 8.7 %collective-permute-start.6 = (bf16[64,2048]{1,0:T(8,128)(2,1)S(1)}, bf16[64,2048]{1,0:T(8,128)(2,1)S(1)}, u32[]{:S(2)}, u32[]{:S(2)}) collective-permute-start(bf16[64,2048]{1,0:T(8,128)(2,1)S(1)} %slice.45), channel_id=1, source_target_pairs={{0,2},{1,3},{2,0},{3,1},{4,6},{5,7},{6,4},{7,5},{8,10},{9,11},{10,... | collective-permute-start | bytes 786440 | tf_op jit(solution)/shard_map/ppermute | solution.py:219
  37.9 9.8 %collective-permute-start.7 = (bf16[16,2048]{1,0:T(8,128)(2,1)S(1)}, bf16[16,2048]{1,0:T(8,128)(2,1)S(1)}, u32[]{:S(2)}, u32[]{:S(2)}) collective-permute-start(bf16[16,2048]{1,0:T(8,128)(2,1)S(1)} %get-tuple-element.14), channel_id=1, source_target_pairs={{0,4},{1,5},{2,6},{3,7},{4,0},{5,1},{6,2},{7,3},{8,12},{9,13},{10,... | collective-permute-start | bytes 196616 | tf_op jit(solution)/shard_map/ppermute | solution.py:219
  39.0 8.7 %collective-permute-start.8 = (bf16[16,2048]{1,0:T(8,128)(2,1)S(1)}, bf16[16,2048]{1,0:T(8,128)(2,1)S(1)}, u32[]{:S(2)}, u32[]{:S(2)}) collective-permute-start(bf16[16,2048]{1,0:T(8,128)(2,1)S(1)} %get-tuple-element.16), channel_id=1, source_target_pairs={{0,8},{1,9},{2,10},{3,11},{4,12},{5,13},{6,14},{7,15},{8,0},{9,1},... | collective-permute-start | bytes 196616 | tf_op jit(solution)/shard_map/ppermute | solution.py:219
  40.5 7.2 %collective-permute-start.9 = (bf16[16,2048]{1,0:T(8,128)(2,1)S(1)}, bf16[16,2048]{1,0:T(8,128)(2,1)S(1)}, u32[]{:S(2)}, u32[]{:S(2)}) collective-permute-start(bf16[16,2048]{1,0:T(8,128)(2,1)S(1)} %get-tuple-element.15), channel_id=1, source_target_pairs={{0,12},{1,13},{2,14},{3,15},{4,8},{5,9},{6,10},{7,11},{8,4},{9,5},... | collective-permute-start | bytes 196616 | tf_op jit(solution)/shard_map/ppermute | solution.py:219
